TPU v7x, 32 devices: a whole 2x2x4 slice. The times are simulated.
32 devices in a mesh: rep: 4 (over x, core), fsdp: 8 (over z, y).
Axes of the slice: x: 2, y: 2, z: 4, core: 2. Of those that a mesh axis runs over, the one named last changes fastest.
Arguments:
- features: bfloat16 [4096, 1280], P(('rep', 'fsdp')), may hold values from -6 to 6
- cotangent: bfloat16 [4096, 1280], P(('rep', 'fsdp')), may hold values from -1 to 1
- clip_lengths: int32 [4, 8], P('rep'), may hold values from 96 to 128, as said below
- group_clips: int32 [4], P('rep'), may hold values from 6 to 8, as said below
- outer_attention: float32 [2, 1280, 5120], P(None, 'fsdp')
- outer_feedforward: float32 [2, 1280, 10240], P(None, 'fsdp')
- outer_vectors: float32 [2, 12, 1280], P(None, None, 'fsdp')
- moments_attention: float32 [4, 2, 1280, 5120], P('rep', None, 'fsdp')
- moments_feedforward: float32 [4, 2, 1280, 10240], P('rep', None, 'fsdp')
- moments_vectors: float32 [4, 2, 12, 1280], P('rep', None, None, 'fsdp')
Outputs:
- block_output: bfloat16 [4096, 1280], P(('rep', 'fsdp'))
- input_grad: float32 [4096, 1280], P(('rep', 'fsdp'))
- group_attention: float32 [4, 3, 1280, 5120], P('rep', None, 'fsdp')
- group_feedforward: float32 [4, 3, 1280, 10240], P('rep', None, 'fsdp')
- group_vectors: float32 [4, 3, 12, 1280], P('rep', None, None, 'fsdp')
- group_weights: float32 [4, 1280, 15372], P('rep', 'fsdp')
- next_attention: float32 [3, 1280, 5120], P(None, 'fsdp')
- next_feedforward: float32 [3, 1280, 10240], P(None, 'fsdp')
- next_vectors: float32 [3, 12, 1280], P(None, None, 'fsdp')
- copy_attention: bfloat16 [1280, 5120], P('fsdp')
- copy_feedforward: bfloat16 [1280, 10240], P('fsdp')
- copy_vectors: bfloat16 [12, 1280], P(None, 'fsdp')
Inputs may be any that keep to these rules, and one draw needn't show every extreme that they name: `clip_lengths`: some clip has exactly 128 valid tokens and some exactly 96. Group g holds clips in its slots 0 to group_clips[g] - 1 and none in the others; some group has all 8 and some 8 - 2.
All inputs are finite; a program needn't handle non-finite values.
Results may differ from a plain program's by a relative error of at most 0.012.
The roundings to bfloat16 on the way count: a program that leaves them out, or rounds other values in their place, can miss the bound.
Values may be sent and summed in bfloat16 or wider, within the bound.
A program may use at most 448 MiB of HBM per device.

v0:
```python
from functools import partial
import jax
import jax.numpy as jnp
from jax import lax
from jax.sharding import PartitionSpec as P

D = 1280
HEADS = 16
HD = 80
FF = 5120
STEP = 3
NORM_EPS = 1e-05
MASKED = -1e30
ADAM_RATE = 0.03
ADAM_DECAY = 0.1
ADAM_BETA = 0.5
ADAM_EPS = 1e-08
OUTER_RATE = 0.7
OUTER_MOMENTUM = 0.5


def contract_last(left, right):
    return lax.dot_general(
        left, right, (((1,), (1,)), ((), ())), preferred_element_type=jnp.float32
    )


def contract_rows(left, right):
    return lax.dot_general(
        left, right, (((0,), (0,)), ((), ())), preferred_element_type=jnp.float32
    )


def normalize(inputs, gain_row, shift_row):
    average = jnp.mean(inputs, axis=-1, keepdims=True)
    centered = inputs - average
    reciprocal = lax.rsqrt(jnp.mean(centered * centered, axis=-1, keepdims=True) + NORM_EPS)
    unit_rows = centered * reciprocal
    return (unit_rows * gain_row + shift_row, unit_rows, reciprocal)


def normalize_back(incoming, unit_rows, reciprocal, gain_row):
    scaled = incoming * gain_row
    centered = scaled - jnp.mean(scaled, axis=-1, keepdims=True)
    return reciprocal * (
        centered - unit_rows * jnp.mean(scaled * unit_rows, axis=-1, keepdims=True)
    )


def adamw_step(weight, gradient, moments, decay_rate):
    first_moment = ADAM_BETA * moments[0] + (1.0 - ADAM_BETA) * gradient
    second_moment = ADAM_BETA * moments[1] + (1.0 - ADAM_BETA) * gradient * gradient
    correction = 1.0 - ADAM_BETA**STEP
    direction = first_moment / correction / (jnp.sqrt(second_moment / correction) + ADAM_EPS)
    return (weight - ADAM_RATE * (direction + decay_rate * weight), first_moment, second_moment)


def outer_step(master, mean_delta, momentum_old):
    momentum = OUTER_MOMENTUM * momentum_old - mean_delta
    outer_next = master - OUTER_RATE * (OUTER_MOMENTUM * momentum - mean_delta)
    return jnp.stack([mean_delta, momentum, outer_next])


def shards(
    features,
    cotangent,
    clip_lengths,
    group_clips,
    outer_attention,
    outer_feedforward,
    outer_vectors,
    moments_attention,
    moments_feedforward,
    moments_vectors,
):
    tokens_here = features.shape[0]
    scale = HD ** (-0.5)
    clip_slot = lax.axis_index("fsdp")
    clip_length = lax.dynamic_index_in_dim(clip_lengths[0], clip_slot, keepdims=False)
    live_clip = clip_slot < group_clips[0]
    positions = jnp.arange(tokens_here, dtype=jnp.int32)
    key_valid = positions < clip_length
    row_valid = key_valid & live_clip
    masters = (outer_attention[0], outer_feedforward[0], outer_vectors[0])
    copies = (
        masters[0].astype(jnp.bfloat16),
        masters[1].astype(jnp.bfloat16),
        masters[2].astype(jnp.bfloat16),
    )
    full_attention, full_feedforward, full_vectors = (
        lax.all_gather(copies[0], "fsdp", axis=0, tiled=True),
        lax.all_gather(copies[1], "fsdp", axis=0, tiled=True),
        lax.all_gather(copies[2], "fsdp", axis=1, tiled=True),
    )
    vectors = full_vectors.astype(jnp.float32)
    inputs = features.astype(jnp.float32)
    normed_one, unit_one, scale_one = normalize(inputs, vectors[0], vectors[1])
    layer_one = normed_one.astype(jnp.bfloat16)
    qkv_bias = jnp.concatenate([vectors[2], jnp.zeros_like(vectors[2]), vectors[3]])
    projected = (
        jnp.dot(layer_one, full_attention[:, : 3 * D], preferred_element_type=jnp.float32)
        + qkv_bias
    ).astype(jnp.bfloat16)
    query_heads = projected[:, :D].reshape(tokens_here, HEADS, HD)
    key_heads = projected[:, D : 2 * D].reshape(tokens_here, HEADS, HD)
    value_heads = projected[:, 2 * D :].reshape(tokens_here, HEADS, HD)

    def score_block():
        raw_scores = (
            jnp.einsum("qhd,khd->hqk", query_heads, key_heads, preferred_element_type=jnp.float32)
            * scale
        )
        return jnp.where(key_valid[None, None, :], raw_scores, MASKED)

    scores = score_block()
    top_score = jnp.max(scores, axis=-1, keepdims=True)
    exponent = jnp.exp(scores - top_score)
    totals = jnp.sum(exponent, axis=-1, keepdims=True)
    attention_probs = exponent / totals
    log_totals = top_score + jnp.log(totals)
    attended = jnp.einsum(
        "hqk,khd->qhd",
        attention_probs.astype(jnp.bfloat16),
        value_heads,
        preferred_element_type=jnp.float32,
    )
    attended = attended.reshape(tokens_here, D).astype(jnp.bfloat16)
    attention_branch = contract_last(attended, full_attention[:, 3 * D :]) + vectors[4]
    middle = inputs + attention_branch
    normed_two, unit_two, scale_two = normalize(middle, vectors[5], vectors[6])
    layer_two = normed_two.astype(jnp.bfloat16)
    pre_activation = jnp.dot(
        layer_two, full_feedforward[:, :FF], preferred_element_type=jnp.float32
    ) + vectors[8:].reshape(FF)
    activation, gelu_backward = jax.vjp(partial(jax.nn.gelu, approximate=False), pre_activation)
    activation_low = activation.astype(jnp.bfloat16)
    feedforward_branch = contract_last(activation_low, full_feedforward[:, FF:]) + vectors[7]
    block_output = (middle + feedforward_branch).astype(jnp.bfloat16)
    back_attention, back_feedforward, back_vectors = (
        lax.all_gather(copies[0], "fsdp", axis=0, tiled=True),
        lax.all_gather(copies[1], "fsdp", axis=0, tiled=True),
        lax.all_gather(copies[2], "fsdp", axis=1, tiled=True),
    )
    gain_rows = back_vectors.astype(jnp.float32)
    upstream = cotangent.astype(jnp.float32) * row_valid[:, None].astype(jnp.float32)
    upstream_low = upstream.astype(jnp.bfloat16)
    grad_down_bias = jnp.sum(upstream_low, axis=0, dtype=jnp.float32)
    grad_activation = jnp.dot(
        upstream_low, back_feedforward[:, FF:], preferred_element_type=jnp.float32
    )
    grad_pre = gelu_backward(grad_activation)[0].astype(jnp.bfloat16)
    grad_up_bias = jnp.sum(grad_pre, axis=0, dtype=jnp.float32)
    grad_two = contract_last(grad_pre, back_feedforward[:, :FF])
    grad_gain_two = jnp.sum(grad_two * unit_two, axis=0)
    grad_shift_two = jnp.sum(grad_two, axis=0)
    grad_middle = upstream + normalize_back(grad_two, unit_two, scale_two, gain_rows[5])
    middle_low = grad_middle.astype(jnp.bfloat16)
    grad_out_bias = jnp.sum(middle_low, axis=0, dtype=jnp.float32)
    grad_attended = jnp.dot(
        middle_low, back_attention[:, 3 * D :], preferred_element_type=jnp.float32
    ).astype(jnp.bfloat16)
    grad_heads = grad_attended.reshape(tokens_here, HEADS, HD)
    attention_probs = jnp.exp(score_block() - log_totals)
    grad_probs = jnp.einsum(
        "qhd,khd->hqk", grad_heads, value_heads, preferred_element_type=jnp.float32
    )
    row_dot = jnp.sum(attention_probs * grad_probs, axis=-1, keepdims=True)
    grad_scores = (attention_probs * (grad_probs - row_dot)).astype(jnp.bfloat16)
    grad_queries = (
        jnp.einsum("hqk,khd->qhd", grad_scores, key_heads, preferred_element_type=jnp.float32)
        * scale
    ).reshape(tokens_here, D)
    grad_keys = (
        jnp.einsum("hqk,qhd->khd", grad_scores, query_heads, preferred_element_type=jnp.float32)
        * scale
    ).reshape(tokens_here, D)
    grad_values = jnp.einsum(
        "hqk,qhd->khd",
        attention_probs.astype(jnp.bfloat16),
        grad_heads,
        preferred_element_type=jnp.float32,
    ).reshape(tokens_here, D)
    grad_qkv = jnp.concatenate([grad_queries, grad_keys, grad_values], axis=1).astype(jnp.bfloat16)
    grad_query_bias = jnp.sum(grad_qkv[:, :D], axis=0, dtype=jnp.float32)
    grad_value_bias = jnp.sum(grad_qkv[:, 2 * D :], axis=0, dtype=jnp.float32)
    grad_one = contract_last(grad_qkv, back_attention[:, : 3 * D])
    grad_gain_one = jnp.sum(grad_one * unit_one, axis=0)
    grad_shift_one = jnp.sum(grad_one, axis=0)
    input_grad = grad_middle + normalize_back(grad_one, unit_one, scale_one, gain_rows[0])
    vector_rows = jnp.stack(
        [
            grad_gain_one,
            grad_shift_one,
            grad_query_bias,
            grad_value_bias,
            grad_out_bias,
            grad_gain_two,
            grad_shift_two,
            grad_down_bias,
        ]
    )
    grad_vectors = jnp.concatenate([vector_rows, grad_up_bias.reshape(4, D)], axis=0)
    owned_attention = lax.psum_scatter(
        jnp.concatenate(
            [contract_rows(layer_one, grad_qkv), contract_rows(middle_low, attended)], axis=1
        ),
        "fsdp",
        scatter_dimension=0,
        tiled=True,
    )
    owned_feedforward = lax.psum_scatter(
        jnp.concatenate(
            [contract_rows(layer_two, grad_pre), contract_rows(upstream_low, activation_low)],
            axis=1,
        ),
        "fsdp",
        scatter_dimension=0,
        tiled=True,
    )
    owned_vectors = lax.psum_scatter(grad_vectors, "fsdp", scatter_dimension=1, tiled=True)
    new_attention, first_attention, second_attention = adamw_step(
        masters[0], owned_attention, moments_attention[0], ADAM_DECAY
    )
    new_feedforward, first_feedforward, second_feedforward = adamw_step(
        masters[1], owned_feedforward, moments_feedforward[0], ADAM_DECAY
    )
    new_vectors, first_vectors, second_vectors = adamw_step(
        masters[2], owned_vectors, moments_vectors[0], 0.0
    )
    summed = (
        lax.psum_scatter(
            (new_attention - masters[0]).astype(jnp.bfloat16),
            "rep",
            scatter_dimension=1,
            tiled=True,
        ).astype(jnp.float32),
        lax.psum_scatter(
            (new_feedforward - masters[1]).astype(jnp.bfloat16),
            "rep",
            scatter_dimension=1,
            tiled=True,
        ).astype(jnp.float32),
        lax.psum_scatter(
            (new_vectors - masters[2]).astype(jnp.bfloat16), "rep", scatter_dimension=0, tiled=True
        ).astype(jnp.float32),
    )
    replicas = lax.axis_size("rep")
    replica_index = lax.axis_index("rep")
    attention_cols = 4 * D // replicas
    feedforward_cols = 2 * FF // replicas
    vector_count = 12 // replicas

    def owned_part(array, dim, count):
        return lax.dynamic_slice_in_dim(array, replica_index * count, count, dim)

    part_attention = outer_step(
        owned_part(masters[0], 1, attention_cols),
        summed[0] / replicas,
        owned_part(outer_attention[1], 1, attention_cols),
    )
    part_feedforward = outer_step(
        owned_part(masters[1], 1, feedforward_cols),
        summed[1] / replicas,
        owned_part(outer_feedforward[1], 1, feedforward_cols),
    )
    part_vectors = outer_step(
        owned_part(masters[2], 0, vector_count),
        summed[2] / replicas,
        owned_part(outer_vectors[1], 0, vector_count),
    )
    next_attention, next_feedforward, next_vectors = (
        lax.all_gather(part_attention, "rep", axis=2, tiled=True),
        lax.all_gather(part_feedforward, "rep", axis=2, tiled=True),
        lax.all_gather(part_vectors, "rep", axis=1, tiled=True),
    )
    copy_attention = next_attention[2].astype(jnp.bfloat16)
    copy_feedforward = next_feedforward[2].astype(jnp.bfloat16)
    copy_vectors = next_vectors[2].astype(jnp.bfloat16)
    group_attention = jnp.stack([owned_attention, first_attention, second_attention])[None]
    group_feedforward = jnp.stack([owned_feedforward, first_feedforward, second_feedforward])[None]
    group_vectors = jnp.stack([owned_vectors, first_vectors, second_vectors])[None]
    group_weights = jnp.concatenate([new_attention, new_feedforward, new_vectors.T], axis=1)[None]
    return (
        block_output,
        input_grad,
        group_attention,
        group_feedforward,
        group_vectors,
        group_weights,
        next_attention,
        next_feedforward,
        next_vectors,
        copy_attention,
        copy_feedforward,
        copy_vectors,
    )


def solution(mesh):
    in_specs = (
        P(("rep", "fsdp"), None),
        P(("rep", "fsdp"), None),
        P("rep", None),
        P("rep"),
        P(None, "fsdp", None),
        P(None, "fsdp", None),
        P(None, None, "fsdp"),
        P("rep", None, "fsdp", None),
        P("rep", None, "fsdp", None),
        P("rep", None, None, "fsdp"),
    )
    out_specs = (
        P(("rep", "fsdp"), None),
        P(("rep", "fsdp"), None),
        P("rep", None, "fsdp", None),
        P("rep", None, "fsdp", None),
        P("rep", None, None, "fsdp"),
        P("rep", "fsdp", None),
        P(None, "fsdp", None),
        P(None, "fsdp", None),
        P(None, None, "fsdp"),
        P("fsdp", None),
        P("fsdp", None),
        P(None, "fsdp"),
    )
    return jax.shard_map(shards, mesh=mesh, in_specs=in_specs, out_specs=out_specs, check_vma=False)
```

profile of v0, /device:TPU:0, one launch (start us, length us, event | category | flops | bytes accessed | tf_op | source)
XLA Modules:
  0.0 2351.6 jit_solution(7769149582330624274)
XLA Ops:
  7.2 3.3 bitcast_convert_fusion.1
  10.6 5.0 bitcast_convert_fusion
  15.7 0.7 copy-done.17
  16.3 0.6 fusion.119
  17.1 33.6 %all-gather = bf16[8,160,12]{1,2,0:T(8,128)(2,1)S(1)} all-gather(bf16[1,160,12]{1,2,0:T(8,128)(2,1)S(1)} %copy.142), channel_id=1, replica_groups=mesh['rep'=4,'fsdp'=8] {'fsdp'}, dimensions={0}, use_global_device_ids=true | all-gather | bytes 34560 | tf_op jit(solution)/shard_map/all_gather | solution.py:93
  51.6 0.6 constant_dynamic-slice_fusion.1
  52.2 0.6 iota_compare_fusion
  52.9 0.7 and_convert_fusion
  53.5 0.7 slice_reduce_fusion.2
  54.6 141.9 %all-gather.6.cloned.1.call-done = bf16[1280,5120]{1,0:T(8,128)(2,1)} async-done(((bf16[160,5120]{1,0:T(8,128)(2,1)}), bf16[1280,5120]{1,0:T(8,128)(2,1)}) %all-gather.6.cloned.1.call-update) | async-done | bytes 13107216 | tf_op jit(solution)/shard_map/all_gather | solution.py:91
  196.5 5.3 fusion.22
  203.5 3.7 fusion.122
  207.5 489.4 %all-gather.8.cloned.1.call-done = bf16[1280,10240]{1,0:T(8,128)(2,1)} async-done(((bf16[160,10240]{1,0:T(8,128)(2,1)}), bf16[1280,10240]{1,0:T(8,128)(2,1)}) %all-gather.8.cloned.1.call-update) | async-done | bytes 26214416 | tf_op jit(solution)/shard_map/all_gather | solution.py:92
  696.8 5.9 fusion.16
  702.8 11.3 convert_reduce_fusion
  714.1 8.4 multiply_reduce_fusion.1
  723.0 3.3 fusion.57
  726.2 1.9 copy.148
  728.1 1.5 convolution_convert_fusion
  729.6 1.6 multiply_reduce_fusion
  732.3 1.0 fusion.107
  733.3 2.9 fusion.93
  736.2 9.2 pad_maximum_fusion.1
  745.6 13.1 fusion.115
  758.6 12.3 fusion.110
  770.9 34.1 %pad_maximum_fusion = f32[1280,10240]{1,0:T(8,128)} fusion(f32[1280,5120]{1,0:T(8,128)} %fusion.110, f32[1280,5120]{1,0:T(8,128)} %fusion.115), kind=kLoop, calls=%fused_computation | loop fusion | flops 13107200 | bytes 104857600 | tf_op jit(solution)/shard_map/concatenate | solution.py:212
  805.1 358.9 %reduce-scatter.7.cloned.1.call-done = f32[160,5120]{1,0:T(8,128)} async-done(((f32[1280,5120]{1,0:T(8,128)}), f32[160,5120]{1,0:T(8,128)}) %reduce-scatter.7.cloned.1.call-update) | async-done | bytes 3276816 | tf_op jit(solution)/shard_map/reduce_scatter | solution.py:203
  1164.0 9.6 fusion.29
  1173.7 811.0 %reduce-scatter.9.cloned.1.call-done = f32[160,10240]{1,0:T(8,128)} async-done(((f32[1280,10240]{1,0:T(8,128)}), f32[160,10240]{1,0:T(8,128)}) %reduce-scatter.9.cloned.1.call-update) | async-done | bytes 6553616 | tf_op jit(solution)/shard_map/reduce_scatter | solution.py:211
  1984.6 18.2 fusion.15
  2003.2 6.5 fusion.117
  2009.7 6.0 fusion.87
  2016.3 1.1 copy.153
  2017.6 1.7 fusion.90
  2019.3 1.7 pad_maximum_fusion.3
  2021.1 12.6 fusion.116
  2033.6 22.6 reduce-scatter.15.cloned.1.call-done
  2056.3 2.8 fusion.66
  2059.1 2.5 pad_maximum_fusion.2
  2061.6 0.7 copy-done.18
  2062.5 0.7 copy.172
  2063.2 0.7 constant_dynamic-slice_fusion
  2064.0 0.6 dynamic-slice.7
  2065.3 1.1 fusion.86
  2066.4 13.2 fusion.54
  2079.6 42.7 %reduce-scatter.11.cloned.1.call-done = f32[12,160]{0,1:T(8,128)} async-done(((f32[12,1280]{0,1:T(8,128)}), f32[12,160]{0,1:T(8,128)}) %reduce-scatter.11.cloned.1.call-update) | async-done | bytes 7696 | tf_op jit(solution)/shard_map/reduce_scatter | solution.py:220
  2122.3 1.7 fusion.98
  2124.0 1.0 copy.158
  2124.9 1.0 copy.157
  2125.9 1.0 copy.156
  2126.9 0.7 copy.162
  2127.6 12.0 all-reduce
  2139.9 5.8 all_gather.26
  2145.7 0.6 fusion.104
  2146.3 8.3 maximum_bitcast_fusion.2
  2154.6 35.4 %all-gather.10.cloned.1.call-done = f32[3,160,5120]{2,1,0:T(8,128)} async-done(((f32[3,160,1280]{2,1,0:T(8,128)}), f32[3,160,5120]{2,1,0:T(8,128)}) %all-gather.10.cloned.1.call-update) | async-done | bytes 9830416 | tf_op jit(solution)/shard_map/all_gather | solution.py:272
  2190.0 3.3 fusion.61
  2193.4 19.0 maximum_bitcast_fusion
  2212.3 0.8 copy-done.3
  2213.1 5.5 maximum_bitcast_fusion.1
  2218.6 97.3 %all-gather.12.cloned.1.call-done = f32[3,160,10240]{2,1,0:T(8,128)} async-done(((f32[3,160,2560]{2,1,0:T(8,128)}), f32[3,160,10240]{2,1,0:T(8,128)}) %all-gather.12.cloned.1.call-update) | async-done | bytes 19660816 | tf_op jit(solution)/shard_map/all_gather | solution.py:273
  2315.8 5.0 fusion.26
  2320.8 8.8 copy.180
  2329.6 15.0 copy.181
  (118 shorter events, 5.9 us)
Async XLA Ops:
  7.2 44.4 %copy-start = (s32[1,8]{1,0:T(1,128)S(1)}, s32[1,8]{1,0:T(1,128)}, u32[]{:S(2)}) copy-start(s32[1,8]{1,0:T(1,128)} %param.12) | copy-start | bytes 100
  7.2 189.3 %all-gather.6.cloned.1.call-start = ((), (), s32[]{:S(2)}) async-start(), calls=%async_computation.5 | async-start | bytes 14745600 | tf_op jit(solution)/shard_map/all_gather | solution.py:91
  10.6 686.3 %all-gather.8.cloned.1.call-start = ((), (), s32[]{:S(2)}) async-start(), calls=%async_computation.6 | async-start | bytes 29491200 | tf_op jit(solution)/shard_map/all_gather | solution.py:92
  15.6 0.7 copy-start.17
  15.6 38.6 %copy-start.5 = (bf16[128,1280]{1,0:T(8,128)(2,1)S(1)}, bf16[128,1280]{1,0:T(8,128)(2,1)}, u32[]{:S(2)}) copy-start(bf16[128,1280]{1,0:T(8,128)(2,1)} %param.10) | copy-start | bytes 983044
  15.6 1148.4 %reduce-scatter.7.cloned.1.call-start = ((), (), s32[]{:S(2)}) async-start(), calls=%async_computation.7 | async-start | bytes 29491200 | tf_op jit(solution)/shard_map/reduce_scatter | solution.py:203
  17.1 184.8 %copy-start.9 = (f32[1,12,160]{1,2,0:T(8,128)}, f32[1,12,160]{1,2,0:T(8,128)S(1)}, u32[]{:S(2)}) copy-start(f32[1,12,160]{1,2,0:T(8,128)S(1)} %copy.171) | copy-start | bytes 23044
  202.1 1.3 copy-start.11
  203.5 3.7 copy-start.12
  207.2 538.3 %copy-start.4 = (f32[128,1280]{1,0:T(8,128)}, f32[128,1280]{1,0:T(8,128)S(1)}, u32[]{:S(2)}) copy-start(f32[128,1280]{1,0:T(8,128)S(1)} %get-tuple-element.138) | copy-start | bytes 1966084
  696.8 5.9 copy-start.14
  702.8 11.3 copy-start.21
  714.1 8.4 copy-start.8
  729.6 3.7 copy-start.6
  731.2 1.1 copy-start.13
  745.5 13.2 copy-start.15
  745.5 1239.1 %reduce-scatter.9.cloned.1.call-start = ((), (), s32[]{:S(2)}) async-start(), calls=%async_computation.8 | async-start | bytes 58982400 | tf_op jit(solution)/shard_map/reduce_scatter | solution.py:211
  745.5 13.1 copy-start.22
  805.0 1212.5 %reduce-scatter.13.cloned.1.call-start = ((), (), s32[]{:S(2)}) async-start(), calls=%async_computation.10 | async-start | bytes 2048000 | tf_op jit(solution)/shard_map/reduce_scatter | solution.py:231
  1173.6 882.6 %reduce-scatter.15.cloned.1.call-start = ((), (), s32[]{:S(2)}) async-start(), calls=%async_computation.12 | async-start | bytes 4096000 | tf_op jit(solution)/shard_map/reduce_scatter | solution.py:237
  2002.9 119.4 %reduce-scatter.11.cloned.1.call-start = ((), (), s32[]{:S(2)}) async-start(), calls=%async_computation.9 | async-start | bytes 737280 | tf_op jit(solution)/shard_map/reduce_scatter | solution.py:220
  2003.2 6.5 copy-start.7
  2017.5 172.6 %all-gather.10.cloned.1.call-start = ((), (), s32[]{:S(2)}) async-start(), calls=%async_computation.11 | async-start | bytes 12288000 | tf_op jit(solution)/shard_map/all_gather | solution.py:272
  2021.0 294.8 %all-gather.12.cloned.1.call-start = ((), (), s32[]{:S(2)}) async-start(), calls=%async_computation.13 | async-start | bytes 24576000 | tf_op jit(solution)/shard_map/all_gather | solution.py:273
  2061.6 0.7 copy-start.18
  2061.6 2.4 copy-start.20
  2061.6 4.8 copy-start.19
  2066.4 55.9 %copy-start.10 = (f32[1,12,160]{1,2,0:T(8,128)S(1)}, f32[1,12,160]{1,2,0:T(8,128)}, u32[]{:S(2)}) copy-start(f32[1,12,160]{1,2,0:T(8,128)} %copy-done.9) | copy-start | bytes 23044
  2066.4 79.9 %copy-start.2 = (f32[160,5120]{1,0:T(8,128)S(1)}, f32[160,5120]{1,0:T(8,128)}, u32[]{:S(2)}) copy-start(f32[160,5120]{1,0:T(8,128)} %reduce-scatter.7.cloned.1.call-done) | copy-start | bytes 9830404
  2145.7 9.0 copy-start.16
  2193.3 19.0 slice-start
  2193.3 19.0 slice-start.1
  2193.3 19.7 copy-start.3
  2329.6 15.0 copy-start.1
Sparse Core Ops, SparseCore 0:
  10.8 185.6 all-gather.5
  198.6 498.2 all-gather.7
  745.6 418.3 reduce-scatter.6
  1167.8 816.8 reduce-scatter.8
  1987.6 27.6 reduce-scatter.12
  2017.7 38.5 reduce-scatter.14
  2059.5 62.7 reduce-scatter.10
  2123.9 66.1 all-gather.9
  2191.6 124.1 all-gather.11
where the time goes:
time: 2360 us; the launch traced here: 2350 us
  waiting for transfers between devices  2000 us (85%)
  other arithmetic  119 us (5%)
  matrix products  91.1 us (4%)
  local copies, waits for them, and re-layouts  74.3 us (3%)
  blocking collectives  51.4 us (2%)
    reduce_scatter x1, waiting for transfers between devices, shards(): lax.psum_scatter(jnp.concatenate([contract_rows(layer_two, grad_pre), con...  811 us
    all_gather x1, waiting for transfers between devices, shards(): lax.all_gather(copies[1], 'fsdp', axis=0, tiled=True)  489 us
    reduce_scatter x1, waiting for transfers between devices, shards(): lax.psum_scatter(jnp.concatenate([contract_rows(layer_one, grad_qkv), con...  359 us
    all_gather x1, waiting for transfers between devices, shards(): lax.all_gather(copies[0], 'fsdp', axis=0, tiled=True)  142 us
    all_gather x1, waiting for transfers between devices, shards(): lax.all_gather(part_feedforward, 'rep', axis=2, tiled=True)  97.3 us
  transfers between devices with their start and end apart: 9, of which 8 were waited for; matrix products, arithmetic and copies ran while one was open for 9% of the time, Pallas kernels for 0%

commit v1 on v0

--- a/solution.py
+++ b/solution.py
@@ -17,6 +17,31 @@
 ADAM_EPS = 1e-08
 OUTER_RATE = 0.7
 OUTER_MOMENTUM = 0.5
+
+
+def targets_follow(a0, link_axis):
+    now = lax.axis_size(link_axis)
+    big, known, arr_out = (now, lax.axis_index(link_axis), a0.shape[2])
+    row_list = [ii * big if j0 == 2 else ii for j0, ii in enumerate(a0.shape)]
+    placed = jnp.zeros(row_list, a0.dtype)
+    raw_out = lax.dynamic_update_slice_in_dim(placed, a0, known * arr_out, axis=2)
+    z_new = carry_out = a0
+    for dev in range(1, big // 2 + 1):
+        mixed_arr = range(big)
+        ready = map(lambda j0: (j0, (j0 + 1) % big), mixed_arr)
+        wide_out = list(ready)
+        z_new = lax.ppermute(z_new, link_axis, wide_out)
+        raw_out = lax.dynamic_update_slice_in_dim(
+            raw_out, z_new, (known - dev) % big * arr_out, axis=2
+        )
+        if 2 * dev < big:
+            moved = map(lambda j0: (j0, (j0 - 1) % big), range(big))
+            r2 = list(moved)
+            carry_out = lax.ppermute(carry_out, link_axis, r2)
+            raw_out = lax.dynamic_update_slice_in_dim(
+                raw_out, carry_out, (known + dev) % big * arr_out, axis=2
+            )
+    return raw_out
 
 
 def contract_last(left, right):
@@ -270,7 +295,7 @@
     )
     next_attention, next_feedforward, next_vectors = (
         lax.all_gather(part_attention, "rep", axis=2, tiled=True),
-        lax.all_gather(part_feedforward, "rep", axis=2, tiled=True),
+        targets_follow(part_feedforward, "rep"),
         lax.all_gather(part_vectors, "rep", axis=1, tiled=True),
     )
     copy_attention = next_attention[2].astype(jnp.bfloat16)

time: 2360 us -> 2330 us (0.987)
  waiting for transfers between devices: 2000 us -> 1960 us
    all_gather x1 -> x0, waiting for transfers between devices: 97.3 us -> none  [shards(): lax.all_gather(part_feedforward, 'rep', axis=2, tiled=True)]
    ppermute x0 -> x3, waiting for transfers between devices: none -> 41.3 us  [the longest x1 41.3 us: targets_follow(): carry_out = lax.ppermute(carry_out, link_axis, r2)]
    all_gather x1, waiting for transfers between devices: 35.4 us -> 62.8 us  [shards(): lax.all_gather(part_attention, 'rep', axis=2, tiled=True)]
  transfers between devices with their start and end apart: 9 -> 11, of which waited for: 8 -> 8; matrix products, arithmetic and copies ran while one was open for 9% -> 9% of each run, Pallas kernels for 0% -> 0%
where the time goes in v1:
time: 2330 us; the launch traced here: 2320 us
  waiting for transfers between devices  1960 us (84%)
  other arithmetic  120 us (5%)
  matrix products  89.2 us (4%)
  local copies, waits for them, and re-layouts  79 us (3%)
  blocking collectives  51.2 us (2%)
    reduce_scatter x1, waiting for transfers between devices, shards(): lax.psum_scatter(jnp.concatenate([contract_rows(layer_two, grad_pre), con...  811 us
    all_gather x1, waiting for transfers between devices, shards(): lax.all_gather(copies[1], 'fsdp', axis=0, tiled=True)  489 us
    reduce_scatter x1, waiting for transfers between devices, shards(): lax.psum_scatter(jnp.concatenate([contract_rows(layer_one, grad_qkv), con...  359 us
    all_gather x1, waiting for transfers between devices, shards(): lax.all_gather(copies[0], 'fsdp', axis=0, tiled=True)  142 us
    all_gather x1, waiting for transfers between devices, shards(): lax.all_gather(part_attention, 'rep', axis=2, tiled=True)  62.8 us
  transfers between devices with their start and end apart: 11, of which 8 were waited for; matrix products, arithmetic and copies ran while one was open for 9% of the time, Pallas kernels for 0%

profile of v1, /device:TPU:0, one launch (start us, length us, event | category | flops | bytes accessed | tf_op | source)
XLA Modules:
  0.0 2318.0 jit_solution(4520872108890022459)
XLA Ops:
  7.2 3.3 bitcast_convert_fusion.1
  10.6 5.0 bitcast_convert_fusion
  15.7 0.7 copy-done.23
  16.3 0.6 fusion.119
  17.1 33.6 %all-gather = bf16[8,160,12]{1,2,0:T(8,128)(2,1)S(1)} all-gather(bf16[1,160,12]{1,2,0:T(8,128)(2,1)S(1)} %copy.142), channel_id=1, replica_groups=mesh['rep'=4,'fsdp'=8] {'fsdp'}, dimensions={0}, use_global_device_ids=true | all-gather | bytes 34560 | tf_op jit(solution)/shard_map/all_gather | solution.py:118
  52.2 0.6 iota_compare_fusion
  52.9 0.7 and_convert_fusion
  53.5 0.7 slice_reduce_fusion.2
  54.6 141.9 %all-gather.5.cloned.1.call-done = bf16[1280,5120]{1,0:T(8,128)(2,1)} async-done(((bf16[160,5120]{1,0:T(8,128)(2,1)}), bf16[1280,5120]{1,0:T(8,128)(2,1)}) %all-gather.5.cloned.1.call-update) | async-done | bytes 13107216 | tf_op jit(solution)/shard_map/all_gather | solution.py:116
  196.5 5.3 fusion.22
  203.5 3.7 fusion.122
  207.5 489.4 %all-gather.7.cloned.1.call-done = bf16[1280,10240]{1,0:T(8,128)(2,1)} async-done(((bf16[160,10240]{1,0:T(8,128)(2,1)}), bf16[1280,10240]{1,0:T(8,128)(2,1)}) %all-gather.7.cloned.1.call-update) | async-done | bytes 26214416 | tf_op jit(solution)/shard_map/all_gather | solution.py:117
  696.8 5.9 fusion.16
  702.8 11.3 convert_reduce_fusion
  714.1 8.4 multiply_reduce_fusion.1
  723.0 3.5 fusion.57
  726.5 1.9 copy.148
  728.3 1.5 convolution_convert_fusion
  729.8 1.6 multiply_reduce_fusion
  732.5 1.0 fusion.107
  733.6 2.9 fusion.93
  736.5 9.2 pad_maximum_fusion.1
  745.8 1.2 copy-done.12
  747.0 11.6 fusion.115
  758.6 12.3 fusion.110
  770.9 34.3 %pad_maximum_fusion = f32[1280,10240]{1,0:T(8,128)} fusion(f32[1280,5120]{1,0:T(8,128)} %fusion.110, f32[1280,5120]{1,0:T(8,128)} %fusion.115), kind=kLoop, calls=%fused_computation | loop fusion | flops 13107200 | bytes 104857600 | tf_op jit(solution)/shard_map/concatenate | solution.py:237
  805.3 358.9 %reduce-scatter.7.cloned.1.call-done = f32[160,5120]{1,0:T(8,128)} async-done(((f32[1280,5120]{1,0:T(8,128)}), f32[160,5120]{1,0:T(8,128)}) %reduce-scatter.7.cloned.1.call-update) | async-done | bytes 3276816 | tf_op jit(solution)/shard_map/reduce_scatter | solution.py:228
  1164.1 9.6 fusion.29
  1173.8 810.6 %reduce-scatter.9.cloned.1.call-done = f32[160,10240]{1,0:T(8,128)} async-done(((f32[1280,10240]{1,0:T(8,128)}), f32[160,10240]{1,0:T(8,128)}) %reduce-scatter.9.cloned.1.call-update) | async-done | bytes 6553616 | tf_op jit(solution)/shard_map/reduce_scatter | solution.py:236
  1984.4 18.2 fusion.15
  2003.0 6.5 fusion.117
  2009.5 6.0 fusion.87
  2016.1 1.1 copy.153
  2017.3 1.7 fusion.90
  2019.1 1.7 pad_maximum_fusion.3
  2021.0 0.7 copy.172
  2021.7 0.7 constant_dynamic-slice_fusion
  2023.8 12.3 fusion.116
  2036.1 19.9 reduce-scatter.15.cloned.1.call-done
  2055.9 2.8 fusion.66
  2058.8 9.5 broadcast_in_dim.56
  2068.3 5.1 pad_maximum_fusion.2
  2073.4 1.1 fusion.86
  2074.6 12.6 fusion.54
  2087.1 34.8 %reduce-scatter.11.cloned.1.call-done = f32[12,160]{0,1:T(8,128)} async-done(((f32[12,1280]{0,1:T(8,128)}), f32[12,160]{0,1:T(8,128)}) %reduce-scatter.11.cloned.1.call-update) | async-done | bytes 7696 | tf_op jit(solution)/shard_map/reduce_scatter | solution.py:245
  2121.9 1.7 fusion.98
  2123.6 1.0 copy.158
  2124.6 1.0 copy.157
  2125.5 1.0 copy.156
  2126.5 0.7 copy.162
  2127.2 12.0 all-reduce
  2139.6 5.5 all_gather.22
  2145.7 8.3 maximum_bitcast_fusion.2
  2154.1 2.1 collective-permute-start.1
  2156.4 62.8 %all-gather.9.cloned.1.call-done = f32[3,160,5120]{2,1,0:T(8,128)} async-done(((f32[3,160,1280]{2,1,0:T(8,128)}), f32[3,160,5120]{2,1,0:T(8,128)}) %all-gather.9.cloned.1.call-update) | async-done | bytes 9830416 | tf_op jit(solution)/shard_map/all_gather | solution.py:297
  2219.2 3.3 fusion.61
  2222.5 17.0 maximum_bitcast_fusion
  2239.5 5.5 maximum_bitcast_fusion.1
  2245.0 5.0 constant_dynamic-update-slice_fusion.2
  2249.9 41.3 %collective-permute-done.1 = f32[3,160,2560]{2,1,0:T(8,128)} collective-permute-done((f32[3,160,2560]{2,1,0:T(8,128)}, f32[3,160,2560]{2,1,0:T(8,128)}, u32[]{:S(2)}, u32[]{:S(2)}) %collective-permute-start.1) | collective-permute-done | bytes 4915232 | tf_op jit(solution)/shard_map/ppermute | solution.py:40
  2291.2 5.4 constant_dynamic-update-slice_fusion.1
  2296.6 5.3 constant_dynamic-update-slice_fusion
  2301.9 5.0 fusion.26
  2306.9 3.9 copy.183
  (145 shorter events, 7.9 us)
Async XLA Ops:
  7.2 44.4 %copy-start = (s32[1,8]{1,0:T(1,128)S(1)}, s32[1,8]{1,0:T(1,128)}, u32[]{:S(2)}) copy-start(s32[1,8]{1,0:T(1,128)} %param.12) | copy-start | bytes 100
  7.2 189.3 %all-gather.5.cloned.1.call-start = ((), (), s32[]{:S(2)}) async-start(), calls=%async_computation.5 | async-start | bytes 14745600 | tf_op jit(solution)/shard_map/all_gather | solution.py:116
  10.6 686.3 %all-gather.7.cloned.1.call-start = ((), (), s32[]{:S(2)}) async-start(), calls=%async_computation.6 | async-start | bytes 29491200 | tf_op jit(solution)/shard_map/all_gather | solution.py:117
  15.6 0.7 copy-start.23
  15.6 38.6 %copy-start.8 = (bf16[128,1280]{1,0:T(8,128)(2,1)S(1)}, bf16[128,1280]{1,0:T(8,128)(2,1)}, u32[]{:S(2)}) copy-start(bf16[128,1280]{1,0:T(8,128)(2,1)} %param.10) | copy-start | bytes 983044
  15.6 1148.5 %reduce-scatter.7.cloned.1.call-start = ((), (), s32[]{:S(2)}) async-start(), calls=%async_computation.7 | async-start | bytes 29491200 | tf_op jit(solution)/shard_map/reduce_scatter | solution.py:228
  17.1 184.8 %copy-start.13 = (f32[1,12,160]{1,2,0:T(8,128)}, f32[1,12,160]{1,2,0:T(8,128)S(1)}, u32[]{:S(2)}) copy-start(f32[1,12,160]{1,2,0:T(8,128)S(1)} %copy.171) | copy-start | bytes 23044
  202.1 1.3 copy-start.15
  203.5 3.7 copy-start.18
  207.2 538.6 %copy-start.6 = (f32[128,1280]{1,0:T(8,128)}, f32[128,1280]{1,0:T(8,128)S(1)}, u32[]{:S(2)}) copy-start(f32[128,1280]{1,0:T(8,128)S(1)} %get-tuple-element.140) | copy-start | bytes 1966084
  696.8 5.9 copy-start.20
  702.8 11.3 copy-start.27
  714.1 8.4 copy-start.11
  723.0 9.5 copy-start.4
  729.8 3.8 copy-start.9
  731.4 1.1 copy-start.19
  732.2 1.4 copy-start.16
  745.7 1.3 copy-start.12
  745.7 12.9 copy-start.21
  745.8 1238.6 %reduce-scatter.9.cloned.1.call-start = ((), (), s32[]{:S(2)}) async-start(), calls=%async_computation.8 | async-start | bytes 58982400 | tf_op jit(solution)/shard_map/reduce_scatter | solution.py:236
  747.0 11.6 copy-start.28
  805.2 1212.1 %reduce-scatter.13.cloned.1.call-start = ((), (), s32[]{:S(2)}) async-start(), calls=%async_computation.10 | async-start | bytes 2048000 | tf_op jit(solution)/shard_map/reduce_scatter | solution.py:256
  1173.8 882.2 %reduce-scatter.15.cloned.1.call-start = ((), (), s32[]{:S(2)}) async-start(), calls=%async_computation.12 | async-start | bytes 4096000 | tf_op jit(solution)/shard_map/reduce_scatter | solution.py:262
  2002.7 119.2 %reduce-scatter.11.cloned.1.call-start = ((), (), s32[]{:S(2)}) async-start(), calls=%async_computation.9 | async-start | bytes 737280 | tf_op jit(solution)/shard_map/reduce_scatter | solution.py:245
  2002.9 6.5 copy-start.10
  2003.0 6.5 copy-start.17
  2017.2 201.9 %all-gather.9.cloned.1.call-start = ((), (), s32[]{:S(2)}) async-start(), calls=%async_computation.11 | async-start | bytes 12288000 | tf_op jit(solution)/shard_map/all_gather | solution.py:297
  2019.1 1.8 copy-start.24
  2020.7 1.8 copy-start.26
  2068.3 5.1 copy-start.5
  2068.3 6.2 copy-start.7
  2068.3 6.2 copy-start.25
  2068.3 6.2 copy-start.29
  2073.4 82.7 %collective-permute-start = (f32[3,160,2560]{2,1,0:T(8,128)}, f32[3,160,2560]{2,1,0:T(8,128)}, u32[]{:S(2)}, u32[]{:S(2)}) collective-permute-start(f32[3,160,2560]{2,1,0:T(8,128)} %get-tuple-element.118), channel_id=1, source_target_pairs={{0,8},{8,16},{16,24},{24,0},{1,9},{9,17},{17,25},{25,1},{2,10},{10... | collective-permute-start | bytes 14745608 | tf_op jit(solution)/shard_map/ppermute | solution.py:33
  2074.5 47.4 %copy-start.14 = (f32[1,12,160]{1,2,0:T(8,128)S(1)}, f32[1,12,160]{1,2,0:T(8,128)}, u32[]{:S(2)}) copy-start(f32[1,12,160]{1,2,0:T(8,128)} %copy-done.13) | copy-start | bytes 23044
  2074.5 71.2 %copy-start.2 = (f32[160,5120]{1,0:T(8,128)S(1)}, f32[160,5120]{1,0:T(8,128)}, u32[]{:S(2)}) copy-start(f32[160,5120]{1,0:T(8,128)} %reduce-scatter.7.cloned.1.call-done) | copy-start | bytes 9830404
  2145.1 9.0 copy-start.22
  2154.1 137.1 %collective-permute-start.1 = (f32[3,160,2560]{2,1,0:T(8,128)}, f32[3,160,2560]{2,1,0:T(8,128)}, u32[]{:S(2)}, u32[]{:S(2)}) collective-permute-start(f32[3,160,2560]{2,1,0:T(8,128)} %get-tuple-element.118), channel_id=1, source_target_pairs={{0,24},{8,0},{16,8},{24,16},{1,25},{9,1},{17,9},{25,17},{2,26},{10... | collective-permute-start | bytes 14745608 | tf_op jit(solution)/shard_map/ppermute | solution.py:40
  2156.1 140.4 %collective-permute-start.2 = (f32[3,160,2560]{2,1,0:T(8,128)}, f32[3,160,2560]{2,1,0:T(8,128)}, u32[]{:S(2)}, u32[]{:S(2)}) collective-permute-start(f32[3,160,2560]{2,1,0:T(8,128)} %collective-permute-done), channel_id=1, source_target_pairs={{0,8},{8,16},{16,24},{24,0},{1,9},{9,17},{17,25},{25,1},{2,10},{10... | collective-permute-start | bytes 14745608 | tf_op jit(solution)/shard_map/ppermute | solution.py:33
  2222.5 17.0 slice-start
  2222.5 17.0 slice-start.1
  2222.5 17.0 copy-start.3
  2291.2 15.6 slice-start.2
  2291.2 15.6 slice-start.3
  2296.6 10.3 slice-start.4
  2306.9 3.9 copy-start.1
Sparse Core Ops, SparseCore 0:
  10.8 185.6 all-gather.4
  198.6 498.2 all-gather.6
  745.9 418.2 reduce-scatter.6
  1167.9 816.4 reduce-scatter.8
  1987.4 27.5 reduce-scatter.12
  2017.3 38.5 reduce-scatter.14
  2059.2 62.6 reduce-scatter.10
  2123.5 95.6 all-gather.8
